TPU v7x, 32 devices: a whole 2x2x4 slice. The times are simulated.
32 devices in a mesh: expert: 8 (over z, y), tensor: 4 (over x, core).
Axes of the slice: x: 2, y: 2, z: 4, core: 2. Of those that a mesh axis runs over, the one named last changes fastest.
Arguments:
- tokens: bfloat16 [1024, 2048], P('expert', 'tensor'), may hold values from -6 to 6
- grad_out: bfloat16 [1024, 2048], P('expert', 'tensor'), may hold values from -6 to 6
- route_weights: float32 [1024, 8], P('expert'), may hold values from 0.02 to 0.5
- expert_ids: int32 [1024, 8], P('expert'), may hold values from 0 to 15, all different within a row; in each aligned block of 128 rows (0 to 127, 128 to 255, ...) at most 96 rows name the same one
- gate_weight: bfloat16 [16, 2048, 768], P('expert', None, 'tensor'), may hold values from -0.125 to 0.125
- up_weight: bfloat16 [16, 2048, 768], P('expert', None, 'tensor'), may hold values from -0.125 to 0.125
- down_weight: bfloat16 [16, 768, 2048], P('expert', 'tensor'), may hold values from -0.21875 to 0.21875
- gate_adapter_first: bfloat16 [16, 2048, 64], P('expert'), may hold values from -0.125 to 0.125
- gate_adapter_second: bfloat16 [16, 64, 768], P('expert', None, 'tensor'), may hold values from -0.75 to 0.75
- up_adapter_first: bfloat16 [16, 2048, 64], P('expert'), may hold values from -0.125 to 0.125
- up_adapter_second: bfloat16 [16, 64, 768], P('expert', None, 'tensor'), may hold values from -0.75 to 0.75
- down_adapter_first: bfloat16 [16, 768, 64], P('expert', 'tensor'), may hold values from -0.21875 to 0.21875
- down_adapter_second: bfloat16 [16, 64, 2048], P('expert'), may hold values from -0.75 to 0.75
Outputs:
- grad_tokens: bfloat16 [1024, 2048], P('expert', 'tensor')
- gate_first_gradient: float32 [16, 2048, 64], P('expert', 'tensor')
- gate_second_gradient: float32 [16, 64, 768], P('expert', None, 'tensor')
- up_first_gradient: float32 [16, 2048, 64], P('expert', 'tensor')
- up_second_gradient: float32 [16, 64, 768], P('expert', None, 'tensor')
- down_first_gradient: float32 [16, 768, 64], P('expert', 'tensor')
- down_second_gradient: float32 [16, 64, 2048], P('expert', None, 'tensor')
Inputs may be any that keep to these rules, and one draw needn't show every extreme that they name: `expert_ids`: each token names 8 different experts. Among the 128 rows of one device no expert is named more than 96 times, a bound that some block reaches.
All inputs are finite; a program needn't handle non-finite values.
Results may differ from a plain program's by a relative error of at most 0.012.
Values may be sent and summed in bfloat16 or wider, within the bound.
A program may use at most 128 MiB of HBM per device.

v0:
```python
import jax
import jax.numpy as jnp
from jax import lax
from jax.sharding import PartitionSpec as P

adapter_scale = 0.5


def slot_positions(expert_ids, experts_all, capacity):
    tok_rows = expert_ids.shape[0]
    numbers = lax.broadcasted_iota(jnp.int32, (1, 1, experts_all), 2)
    picked = jnp.sum((expert_ids[:, :, None] == numbers).astype(jnp.float32), axis=1).astype(
        jnp.bfloat16
    )
    row_index = lax.broadcasted_iota(jnp.int32, (tok_rows, tok_rows), 0)
    col_index = lax.broadcasted_iota(jnp.int32, (tok_rows, tok_rows), 1)
    earlier = (row_index > col_index).astype(jnp.bfloat16)
    before = jnp.dot(earlier, picked, preferred_element_type=jnp.float32)
    slot_index = jnp.take_along_axis(before, expert_ids, axis=1).astype(jnp.int32)
    return expert_ids * capacity + slot_index


def fill_slots(values, positions, slot_count):
    width = values.shape[-1]
    flat = values.reshape(-1, width)
    return jnp.zeros((slot_count, width), values.dtype).at[positions.reshape(-1)].set(flat)


def local(
    tokens,
    grad_out,
    route_weights,
    expert_ids,
    gate_weight,
    up_weight,
    down_weight,
    gate_adapter_first,
    gate_adapter_second,
    up_adapter_first,
    up_adapter_second,
    down_adapter_first,
    down_adapter_second,
):
    single_float = jnp.float32
    brain_float_half = jnp.bfloat16
    tok_rows, top_count = expert_ids.shape
    local_experts = gate_weight.shape[0]
    sources = lax.axis_size("expert")
    experts_all = local_experts * sources
    capacity = 3 * tok_rows * top_count // (2 * experts_all)
    slot_count = experts_all * capacity
    positions = slot_positions(expert_ids, experts_all, capacity)
    width = tokens.shape[1]
    spread_in = jnp.broadcast_to(tokens[:, None, :], (tok_rows, top_count, width))
    scaled = (route_weights[:, :, None] * grad_out[:, None, :].astype(single_float)).astype(
        brain_float_half
    )
    send_in = fill_slots(spread_in, positions, slot_count)
    send_grad = fill_slots(scaled, positions, slot_count)
    part_in, part_grad = (
        lax.all_to_all(send_in, "expert", split_axis=0, concat_axis=0, tiled=True),
        lax.all_to_all(send_grad, "expert", split_axis=0, concat_axis=0, tiled=True),
    )
    recv_in, recv_grad = (
        lax.all_gather(part_in, "tensor", axis=1, tiled=True),
        lax.all_gather(part_grad, "tensor", axis=1, tiled=True),
    )
    hidden_width = recv_in.shape[1]
    routed_input = recv_in.reshape(sources, local_experts, capacity, hidden_width)
    routed_gradient = recv_grad.reshape(sources, local_experts, capacity, hidden_width)
    slice_width = hidden_width // lax.axis_size("tensor")
    slice_start = lax.axis_index("tensor") * slice_width
    adapter_gate_term = jnp.einsum(
        "mbtk,bkz->mbtz", routed_input, gate_adapter_first, preferred_element_type=single_float
    ).astype(brain_float_half)
    adapter_up_term = jnp.einsum(
        "mbtk,bkz->mbtz", routed_input, up_adapter_first, preferred_element_type=single_float
    ).astype(brain_float_half)
    gate_activation = jnp.einsum(
        "secd,edf->secf", routed_input, gate_weight, preferred_element_type=single_float
    )
    gate_activation = gate_activation + adapter_scale * jnp.einsum(
        "imal,mlt->imat",
        adapter_gate_term,
        gate_adapter_second,
        preferred_element_type=single_float,
    )
    up_activation = jnp.einsum(
        "secd,edf->secf", routed_input, up_weight, preferred_element_type=single_float
    )
    up_activation = up_activation + adapter_scale * jnp.einsum(
        "imal,mlt->imat", adapter_up_term, up_adapter_second, preferred_element_type=single_float
    )
    sigma = jax.nn.sigmoid(gate_activation)
    active = gate_activation * sigma
    hidden_activation = (active * up_activation).astype(brain_float_half)
    down_part = jnp.einsum(
        "secf,efr->secr", hidden_activation, down_adapter_first, preferred_element_type=single_float
    )
    down_total = lax.psum(down_part.astype(jnp.bfloat16), "tensor").astype(jnp.float32)
    backward_adapter_term = jnp.einsum(
        "secd,erd->secr", routed_gradient, down_adapter_second, preferred_element_type=single_float
    ).astype(brain_float_half)
    hidden_gradient = jnp.einsum(
        "secd,efd->secf", routed_gradient, down_weight, preferred_element_type=single_float
    )
    hidden_gradient = hidden_gradient + adapter_scale * jnp.einsum(
        "oamh,ath->oamt",
        backward_adapter_term,
        down_adapter_first,
        preferred_element_type=single_float,
    )
    gate_gradient = (
        hidden_gradient * up_activation * sigma * (1.0 + gate_activation * (1.0 - sigma))
    ).astype(brain_float_half)
    upward_gradient = (hidden_gradient * active).astype(brain_float_half)
    gate_part = jnp.einsum(
        "secf,erf->secr", gate_gradient, gate_adapter_second, preferred_element_type=single_float
    )
    up_part = jnp.einsum(
        "secf,erf->secr", upward_gradient, up_adapter_second, preferred_element_type=single_float
    )
    joined_weight = jnp.concatenate(
        (gate_weight, up_weight, gate_adapter_first, up_adapter_first), axis=2
    )
    joined_grad = jnp.concatenate(
        (
            gate_gradient,
            upward_gradient,
            gate_part.astype(brain_float_half) * adapter_scale,
            up_part.astype(brain_float_half) * adapter_scale,
        ),
        axis=3,
    )
    input_portion = (
        jnp.einsum(
            "secf,edf->secd", joined_grad, joined_weight, preferred_element_type=single_float
        )
        .astype(brain_float_half)
        .reshape(slot_count, hidden_width)
    )
    gate_total, up_total = (
        lax.psum(gate_part.astype(jnp.bfloat16), "tensor").astype(jnp.float32),
        lax.psum(up_part.astype(jnp.bfloat16), "tensor").astype(jnp.float32),
    )
    in_slice = lax.dynamic_slice_in_dim(routed_input, slice_start, slice_width, 3)
    grad_slice = lax.dynamic_slice_in_dim(routed_gradient, slice_start, slice_width, 3)
    gate_first_gradient = adapter_scale * jnp.einsum(
        "secd,secr->edr",
        in_slice,
        gate_total.astype(brain_float_half),
        preferred_element_type=single_float,
    )
    up_first_gradient = adapter_scale * jnp.einsum(
        "secd,secr->edr",
        in_slice,
        up_total.astype(brain_float_half),
        preferred_element_type=single_float,
    )
    gate_second_gradient = adapter_scale * jnp.einsum(
        "zdbq,zdbx->dqx", adapter_gate_term, gate_gradient, preferred_element_type=single_float
    )
    up_second_gradient = adapter_scale * jnp.einsum(
        "zdbq,zdbx->dqx", adapter_up_term, upward_gradient, preferred_element_type=single_float
    )
    down_first_gradient = adapter_scale * jnp.einsum(
        "qoax,qoap->oxp",
        hidden_activation,
        backward_adapter_term,
        preferred_element_type=single_float,
    )
    down_second_gradient = adapter_scale * jnp.einsum(
        "secr,secd->erd",
        down_total.astype(brain_float_half),
        grad_slice,
        preferred_element_type=single_float,
    )
    reduced = lax.psum_scatter(
        input_portion.astype(single_float).astype(jnp.bfloat16),
        "tensor",
        scatter_dimension=1,
        tiled=True,
    ).astype(jnp.float32)
    returned = lax.all_to_all(
        reduced.astype(jnp.bfloat16), "expert", split_axis=0, concat_axis=0, tiled=True
    ).astype(reduced.dtype)
    grad_tokens = jnp.sum(returned[positions], axis=1).astype(brain_float_half)
    return (
        grad_tokens,
        gate_first_gradient,
        gate_second_gradient,
        up_first_gradient,
        up_second_gradient,
        down_first_gradient,
        down_second_gradient,
    )


def solution(mesh):
    return jax.shard_map(
        local,
        mesh=mesh,
        in_specs=(
            P("expert", "tensor"),
            P("expert", "tensor"),
            P("expert", None),
            P("expert", None),
            P("expert", None, "tensor"),
            P("expert", None, "tensor"),
            P("expert", "tensor", None),
            P("expert", None, None),
            P("expert", None, "tensor"),
            P("expert", None, None),
            P("expert", None, "tensor"),
            P("expert", "tensor", None),
            P("expert", None, None),
        ),
        out_specs=(
            P("expert", "tensor"),
            P("expert", "tensor", None),
            P("expert", None, "tensor"),
            P("expert", "tensor", None),
            P("expert", None, "tensor"),
            P("expert", "tensor", None),
            P("expert", None, "tensor"),
        ),
        check_vma=False,
    )
```

profile of v0, /device:TPU:0, one launch (start us, length us, event | category | flops | bytes accessed | tf_op | source)
XLA Modules:
  0.0 321.8 jit_solution(6364558677875069623)
XLA Ops:
  7.2 0.0 copy-start
  7.2 0.0 all-gather.5.cloned.1.call-start
  7.2 0.8 bitcast_or_fusion
  8.0 0.7 convert_reduce_fusion
  8.7 0.1 copy.84
  8.8 0.1 reshape.99
  8.9 0.1 fusion.80
  9.1 7.0 %gather_fusion.1 = f32[1024]{0:T(1024)S(1)} fusion(f32[128,16]{0,1:T(8,128)S(1)} %fusion.80, s32[1024]{0:T(1024)S(1)} %reshape.99), kind=kCustom, calls=%fused_computation.1 | custom fusion | bytes 16384 | tf_op jit(solution)/shard_map/jit(take_along_axis)/gather | solution.py:19
  16.1 0.1 reshape.102
  16.3 0.1 copy.86
  16.4 0.1 reshape.85
  16.5 5.6 %scatter_custom_fusion.1 = bf16[1536,512]{1,0:T(8,128)(2,1)S(1)} fusion(s32[1024]{0:T(1024)S(1)} %bitcast.192, bf16[]{:T(256)} %constant.14.clone.1, bf16[128,512]{1,0:T(8,128)(2,1)S(1)} %copy-done.15), kind=kCustom, calls=%fused_computation.78 | custom fusion | bytes 1703938 | tf_op jit(solution)/shard_map/scatter | solution.py:26
  22.1 0.0 copy-start.19
  22.1 44.3 %all_to_all.33 = bf16[8,192,512]{2,1,0:T(8,128)(2,1)} all-to-all(bf16[8,192,512]{2,1,0:T(8,128)(2,1)S(1)} %bitcast.190), channel_id=1, replica_groups=mesh['expert'=8,'tensor'=4] {'expert'}, dimensions={0} | all-to-all | bytes 3145728 | tf_op jit(solution)/shard_map/all_to_all | solution.py:61
  66.4 0.0 all-gather.5.cloned.1.call-update
  66.5 0.0 all-gather.3.cloned.1.call-start
  66.6 0.1 copy.87
  66.7 0.1 mul.92
  66.8 6.0 %scatter_custom_fusion = bf16[1536,512]{1,0:T(8,128)(2,1)S(1)} fusion(s32[1024]{0:T(1024)S(1)} %bitcast.193, f32[128,512]{1,0:T(8,128)S(1)} %convert_element_type.93, f32[1024]{0:T(1024)S(1)} %mul.92, bf16[]{:T(256)} %constant.14.clone.1), kind=kCustom, calls=%fused_computation.77 | custom fusion | flops 1048576 | bytes 1839106 | tf_op jit(solution)/shard_map/scatter | solution.py:26
  72.7 40.2 %all_to_all.34 = bf16[8,192,512]{2,1,0:T(8,128)(2,1)} all-to-all(bf16[8,192,512]{2,1,0:T(8,128)(2,1)S(1)} %bitcast.189), channel_id=1, replica_groups=mesh['expert'=8,'tensor'=4] {'expert'}, dimensions={0} | all-to-all | bytes 3145728 | tf_op jit(solution)/shard_map/all_to_all | solution.py:62
  112.9 0.0 all-gather.3.cloned.1.call-update
  113.0 0.0 reduce-scatter.2.cloned.1.call-start
  113.0 1.3 copy-done.3
  114.3 2.5 copy.80
  116.8 3.7 %copy.81 = bf16[2,2048,192]{2,1,0:T(8,128)(2,1)} copy(bf16[2,2048,192]{1,2,0:T(8,128)(2,1)} %param.18) | data formatting | bytes 3145728 | tf_op args[5]
  120.5 2.5 copy.82
  123.0 2.5 copy.83
  125.5 5.4 %fusion.37 = bf16[8,2,96,64]{2,3,0,1:T(8,128)(2,1)S(1)} fusion(bf16[2,2048,64]{1,2,0:T(8,128)(2,1)} %param.20, bf16[8,2,96,2048]{3,2,1,0:T(8,128)(2,1)} %bitcast.194), kind=kOutput, calls=%fused_computation.61 | convolution fusion | flops 402751488 | bytes 7012352 | tf_op jit(solution)/shard_map/mbtk,bkz->mbtz/dot_general | solution.py:73
  130.9 3.1 fusion.36
  134.0 3.1 fusion.14
  137.1 3.0 fusion.16
  140.1 19.9 %all-gather.3.cloned.1.call-done = bf16[1536,2048]{1,0:T(8,128)(2,1)} async-done(((bf16[1536,512]{1,0:T(8,128)(2,1)}), bf16[1536,2048]{1,0:T(8,128)(2,1)}) %all-gather.3.cloned.1.call-update) | async-done | bytes 6291472 | tf_op jit(solution)/shard_map/all_gather | solution.py:66
  159.9 5.3 %fusion.35 = bf16[8,2,96,64]{2,3,0,1:T(8,128)(2,1)S(1)} fusion(bf16[2,64,2048]{2,1,0:T(8,128)(2,1)S(1)} %copy-done.22, bf16[8,2,96,2048]{3,2,1,0:T(8,128)(2,1)} %bitcast.200), kind=kOutput, calls=%fused_computation.59 | convolution fusion | flops 402751488 | bytes 7012352 | tf_op jit(solution)/shard_map/secd,erd->secr/dot_general | solution.py:101
  165.3 1.8 fusion.18
  167.2 0.4 multiply_add_fusion
  167.6 0.4 copy-done.12
  168.0 0.4 multiply_add_fusion.2
  168.4 0.5 copy-done.13
  169.0 0.6 copy-done.25
  169.6 1.3 fusion.27
  170.9 1.2 broadcast_multiply_fusion
  172.1 1.2 broadcast_multiply_fusion.1
  173.3 1.9 copy.94
  175.2 1.9 copy.95
  177.1 8.9 %convert_bitcast_fusion = bf16[8,2,96,2048]{3,2,0,1:T(8,128)(2,1)} fusion(bf16[2,2048,64]{2,1,0:T(8,128)(2,1)} %copy.83, bf16[2,2048,64]{2,1,0:T(8,128)(2,1)S(1)} %copy-done.6, bf16[2,2048,192]{2,1,0:T(8,128)(2,1)} %copy.81, bf16[2,2048,192]{2,1,0:T(8,128)(2,1)} %copy.80, bf16[8,2,96,64]{3,2,0,1:T(8,128)(2,1)} %copy.95, bf16[8,2,96,64]{3,2,0,1:T(8,128)(2,1)} %copy.94, ...), kind=kOutput, calls=%fused_computation.4 | convolution fusion | flops 3247439872 | bytes 12058624 | tf_op jit(solution)/shard_map/secf,edf->secd/dot_general | solution.py:136
  186.0 6.6 %copy.96 = bf16[8,2,96,2048]{3,2,1,0:T(8,128)(2,1)} copy(bf16[8,2,96,2048]{3,2,0,1:T(8,128)(2,1)} %convert_bitcast_fusion) | data formatting | bytes 12582912 | tf_op jit(solution)/shard_map/convert_element_type | solution.py:139
  192.6 0.0 reduce-scatter.2.cloned.1.call-update
  192.6 58.0 %reduce-scatter.2.cloned.1.call-done = bf16[1536,512]{1,0:T(8,128)(2,1)} async-done(((bf16[1536,2048]{1,0:T(8,128)(2,1)}), bf16[1536,512]{1,0:T(8,128)(2,1)}) %reduce-scatter.2.cloned.1.call-update) | async-done | bytes 1572880 | tf_op jit(solution)/shard_map/reduce_scatter | solution.py:178
  250.6 5.6 %all-to-all-start.2 = ((bf16[8,192,512]{2,1,0:T(8,128)(2,1)}), bf16[8,192,512]{2,1,0:T(8,128)(2,1)S(1)}, u32[]{:S(2)}, u32[]{:S(2)}) async-start(bf16[8,192,512]{2,1,0:T(8,128)(2,1)} %bitcast.191), calls=%async_computation.3 | async-start | bytes 3145728 | tf_op jit(solution)/shard_map/all_to_all | solution.py:184
  256.3 0.0 all-reduce.3.cloned.1.call-start
  256.3 0.1 copy.97
  256.4 0.1 reshape.93
  256.5 1.1 fusion.40
  257.6 0.0 all-reduce.3.cloned.1.call-update
  257.7 2.1 fusion.59
  259.8 1.9 fusion.60
  261.7 1.0 fusion.61
  262.7 32.6 %all-reduce.3.cloned.1.call-done = (bf16[8,2,96,64]{2,3,0,1:T(8,128)(2,1)}, bf16[8,2,96,64]{2,3,0,1:T(8,128)(2,1)}, bf16[8,2,96,64]{2,3,0,1:T(8,128)(2,1)}) async-done(((bf16[8,2,96,64]{2,3,0,1:T(8,128)(2,1)}, bf16[8,2,96,64]{2,3,0,1:T(8,128)(2,1)}, bf16[8,2,96,64]{2,3,0,1:T(8,128)(2,1)}), (bf16[8,2,96,64]{2,3,0,1:T(8,128)(2,1)}, bf16[8,2,96,64]{2,3,0,1:T(8,128)(2,1)}, ...) | async-done | bytes 589840 | tf_op jit(solution)/shard_map/psum | solution.py:143
  295.2 2.7 fusion.50
  297.9 2.6 fusion.56
  300.5 2.5 fusion.53
  303.0 2.2 bitcast_convert_fusion
  305.2 7.3 %gather_fusion = f32[1024,512]{1,0:T(8,128)} fusion(f32[1536,512]{1,0:T(8,128)} %bitcast_convert_fusion, s32[1024]{0:T(1024)S(1)} %broadcast_clamp_fusion), kind=kCustom, calls=%fused_computation | custom fusion | bytes 4198400 | tf_op jit(solution)/shard_map/gather | solution.py:187
  312.5 2.8 bitcast_reduce_fusion
  (53 shorter events, 0.2 us)
Async XLA Ops:
  7.2 158.1 %copy-start = (bf16[2,192,2048]{2,1,0:T(8,128)(2,1)S(1)}, bf16[2,192,2048]{2,1,0:T(8,128)(2,1)}, u32[]{:S(2)}) copy-start(bf16[2,192,2048]{2,1,0:T(8,128)(2,1)} %param.19) | copy-start | bytes 4718596
  7.2 118.3 %all-gather.5.cloned.1.call-start = ((), (), s32[]{:S(2)}) async-start(), calls=%async_computation.5 | async-start | bytes 7864320 | tf_op jit(solution)/shard_map/all_gather | solution.py:65
  9.1 7.2 %copy-start.18 = (s32[128,8]{0,1:T(8,128)S(1)}, s32[128,8]{0,1:T(8,128)}, u32[]{:S(2)}) copy-start(s32[128,8]{0,1:T(8,128)} %param.16) | copy-start | bytes 12292
  9.1 7.4 %copy-start.15 = (bf16[128,512]{1,0:T(8,128)(2,1)S(1)}, bf16[128,512]{1,0:T(8,128)(2,1)}, u32[]{:S(2)}) copy-start(bf16[128,512]{1,0:T(8,128)(2,1)} %param.13) | copy-start | bytes 393220
  22.1 44.4 %copy-start.16 = (bf16[128,512]{1,0:T(8,128)(2,1)S(1)}, bf16[128,512]{1,0:T(8,128)(2,1)}, u32[]{:S(2)}) copy-start(bf16[128,512]{1,0:T(8,128)(2,1)} %param.14) | copy-start | bytes 393220
  22.1 44.5 %copy-start.19 = (f32[128,8]{0,1:T(8,128)S(1)}, f32[128,8]{0,1:T(8,128)}, u32[]{:S(2)}) copy-start(f32[128,8]{0,1:T(8,128)} %param.15) | copy-start | bytes 12292
  66.5 93.5 %all-gather.3.cloned.1.call-start = ((), (), s32[]{:S(2)}) async-start(), calls=%async_computation.4 | async-start | bytes 7864320 | tf_op jit(solution)/shard_map/all_gather | solution.py:66
  112.9 1.4 copy-start.3
  113.0 137.7 %reduce-scatter.2.cloned.1.call-start = ((), (), s32[]{:S(2)}) async-start(), calls=%async_computation.6 | async-start | bytes 7864320 | tf_op jit(solution)/shard_map/reduce_scatter | solution.py:178
  125.5 5.4 %copy-start.11 = (bf16[2,2048,64]{1,2,0:T(8,128)(2,1)S(1)}, bf16[2,2048,64]{1,2,0:T(8,128)(2,1)}, u32[]{:S(2)}) copy-start(bf16[2,2048,64]{1,2,0:T(8,128)(2,1)} %param.22) | copy-start | bytes 1572868
  125.5 5.4 %copy-start.20 = (bf16[1536,2048]{1,0:T(8,128)(2,1)S(1)}, bf16[1536,2048]{1,0:T(8,128)(2,1)}, u32[]{:S(2)}) copy-start(bf16[1536,2048]{1,0:T(8,128)(2,1)} %all-gather.5.cloned.1.call-done) | copy-start | bytes 18874372
  130.9 36.2 %copy-start.7 = (bf16[8,2,96,64]{2,3,0,1:T(8,128)(2,1)}, bf16[8,2,96,64]{2,3,0,1:T(8,128)(2,1)S(1)}, u32[]{:S(2)}) copy-start(bf16[8,2,96,64]{2,3,0,1:T(8,128)(2,1)S(1)} %fusion.37) | copy-start | bytes 589828
  134.0 3.1 copy-start.4
  137.1 22.8 %copy-start.22 = (bf16[2,64,2048]{2,1,0:T(8,128)(2,1)S(1)}, bf16[2,64,2048]{2,1,0:T(8,128)(2,1)}, u32[]{:S(2)}) copy-start(bf16[2,64,2048]{2,1,0:T(8,128)(2,1)} %param.25) | copy-start | bytes 1572868
  159.9 5.3 %copy-start.21 = (bf16[1536,2048]{1,0:T(8,128)(2,1)S(1)}, bf16[1536,2048]{1,0:T(8,128)(2,1)}, u32[]{:S(2)}) copy-start(bf16[1536,2048]{1,0:T(8,128)(2,1)} %all-gather.3.cloned.1.call-done) | copy-start | bytes 18874372
  165.3 2.3 copy-start.9
  165.3 1.9 copy-start.5
  165.3 1.9 copy-start.14
  167.2 0.8 copy-start.12
  168.0 0.9 copy-start.13
  168.0 1.0 copy-start.17
  168.0 1.5 copy-start.25
  170.9 15.2 %copy-start.2 = (bf16[8,2,96,192]{3,2,0,1:T(8,128)(2,1)}, bf16[8,2,96,192]{3,2,0,1:T(8,128)(2,1)S(1)}, u32[]{:S(2)}) copy-start(bf16[8,2,96,192]{3,2,0,1:T(8,128)(2,1)S(1)} %get-tuple-element.13) | copy-start | bytes 1769476
  170.9 6.2 %copy-start.6 = (bf16[2,2048,64]{2,1,0:T(8,128)(2,1)S(1)}, bf16[2,2048,64]{2,1,0:T(8,128)(2,1)}, u32[]{:S(2)}) copy-start(bf16[2,2048,64]{2,1,0:T(8,128)(2,1)} %copy.82) | copy-start | bytes 1572868
  250.6 7.0 %copy-start.8 = (bf16[8,2,96,64]{2,3,0,1:T(8,128)(2,1)S(1)}, bf16[8,2,96,64]{2,3,0,1:T(8,128)(2,1)}, u32[]{:S(2)}) copy-start(bf16[8,2,96,64]{2,3,0,1:T(8,128)(2,1)} %copy-done.7) | copy-start | bytes 589828
  250.6 52.4 %all-to-all-start.2 = ((bf16[8,192,512]{2,1,0:T(8,128)(2,1)}), bf16[8,192,512]{2,1,0:T(8,128)(2,1)S(1)}, u32[]{:S(2)}, u32[]{:S(2)}) async-start(bf16[8,192,512]{2,1,0:T(8,128)(2,1)} %bitcast.191), calls=%async_computation.3 | async-start | bytes 3145728 | tf_op jit(solution)/shard_map/all_to_all | solution.py:184
  256.3 39.0 %all-reduce.3.cloned.1.call-start = ((), (), s32[]{:S(2)}) async-start(), calls=%async_computation.7 | async-start | bytes 1572864 | tf_op jit(solution)/shard_map/psum | solution.py:143
  257.7 4.0 %copy-start.10 = (bf16[8,2,96,64]{2,3,0,1:T(8,128)(2,1)S(1)}, bf16[8,2,96,64]{2,3,0,1:T(8,128)(2,1)}, u32[]{:S(2)}) copy-start(bf16[8,2,96,64]{2,3,0,1:T(8,128)(2,1)} %copy-done.9) | copy-start | bytes 589828
  295.2 2.7 copy-start.24
  297.9 2.6 copy-start.23
  305.2 10.1 %copy-start.1 = (bf16[2,192,2048]{2,1,0:T(8,128)(2,1)S(1)}, bf16[2,192,2048]{2,1,0:T(8,128)(2,1)}, u32[]{:S(2)}) copy-start(bf16[2,192,2048]{2,1,0:T(8,128)(2,1)} %param.19) | copy-start | bytes 4718596
Sparse Core Ops, SparseCore 0:
  66.6 45.3 all-gather.4
  113.6 46.3 all-gather.2
  192.7 57.8 reduce-scatter.1
  259.9 35.3 all-reduce.2
where the time goes:
time: 323 us; the launch traced here: 322 us
  waiting for transfers between devices  110 us (34%)
  blocking collectives  84.5 us (26%)
  matrix products  49.2 us (15%)
  local copies, waits for them, and re-layouts  45.3 us (14%)
  between operations  14.1 us (4%)
  other arithmetic  12.5 us (4%)
  starting transfers between devices  5.81 us (2%)
    reduce_scatter x1, waiting for transfers between devices, local(): lax.psum_scatter(input_portion.astype(single_float).astype(jnp.bfloat16),...  58 us
    all_to_all x1, blocking collectives, local(): lax.all_to_all(send_in, 'expert', split_axis=0, concat_axis=0, tiled=True)  44.3 us
    all_to_all x1, blocking collectives, local(): lax.all_to_all(send_grad, 'expert', split_axis=0, concat_axis=0, tiled=True)  40.2 us
    psum x1, waiting for transfers between devices, local(): lax.psum(gate_part.astype(jnp.bfloat16), 'tensor').astype(jnp.float32)  32.6 us
    all_gather x1, waiting for transfers between devices, local(): lax.all_gather(part_grad, 'tensor', axis=1, tiled=True)  19.9 us
    unnamed x57, local copies, waits for them, and re-layouts  14.2 us
    dot_general x1, matrix products, local(): jnp.einsum('secf,edf->secd', joined_grad, joined_weight, preferred_elemen...  8.95 us
    gather x5, local copies, waits for them, and re-layouts, slot_positions(): jnp.take_along_axis(before, expert_ids, axis=1).astype(jnp.int32)  7.36 us
  transfers between devices with their start and end apart: 5, of which 3 were waited for; matrix products, arithmetic and copies ran while one was open for 14% of the time, Pallas kernels for 0%

commit v1 on v0

--- a/solution.py
+++ b/solution.py
@@ -4,6 +4,11 @@
 from jax.sharding import PartitionSpec as P
 
 adapter_scale = 0.5
+
+
+def get_the_goods(patch, shard_axis, array_dim):
+    e_now = lax.all_gather(patch, axis_name=shard_axis)
+    return jnp.concatenate(e_now, axis=array_dim)
 
 
 def slot_positions(expert_ids, experts_all, capacity):
@@ -63,7 +68,7 @@
     )
     recv_in, recv_grad = (
         lax.all_gather(part_in, "tensor", axis=1, tiled=True),
-        lax.all_gather(part_grad, "tensor", axis=1, tiled=True),
+        get_the_goods(part_grad, "tensor", array_dim=1),
     )
     hidden_width = recv_in.shape[1]
     routed_input = recv_in.reshape(sources, local_experts, capacity, hidden_width)

time: 323 us -> 342 us (1.059)
  local copies, waits for them, and re-layouts: 45.3 us -> 64 us
    another operation x0 -> x1, local copies, waits for them, and re-layouts: none -> 11.2 us  [local(): recv_grad.reshape(sources, local_experts, capacity, hidden_width)]
    reshape x0 -> x1, local copies, waits for them, and re-layouts: none -> 10.4 us  [get_the_goods(): return jnp.concatenate(e_now, axis=array_dim)]
    unnamed x57 -> x51, local copies, waits for them, and re-layouts: 14.2 us -> 14 us
where the time goes in v1:
time: 342 us; the launch traced here: 341 us
  waiting for transfers between devices  111 us (32%)
  blocking collectives  84.5 us (25%)
  local copies, waits for them, and re-layouts  64 us (19%)
  matrix products  49.1 us (14%)
  between operations  14 us (4%)
  other arithmetic  12.5 us (4%)
  starting transfers between devices  5.85 us (2%)
    reduce_scatter x1, waiting for transfers between devices, local(): lax.psum_scatter(input_portion.astype(single_float).astype(jnp.bfloat16),...  58 us
    all_to_all x1, blocking collectives, local(): lax.all_to_all(send_in, 'expert', split_axis=0, concat_axis=0, tiled=True)  44.3 us
    all_to_all x1, blocking collectives, local(): lax.all_to_all(send_grad, 'expert', split_axis=0, concat_axis=0, tiled=True)  40.2 us
    psum x1, waiting for transfers between devices, local(): lax.psum(gate_part.astype(jnp.bfloat16), 'tensor').astype(jnp.float32)  32.6 us
    all_gather x1, waiting for transfers between devices, get_the_goods(): e_now = lax.all_gather(patch, axis_name=shard_axis)  19.9 us
    unnamed x51, local copies, waits for them, and re-layouts  14 us
    another operation x1, local copies, waits for them, and re-layouts, local(): recv_grad.reshape(sources, local_experts, capacity, hidden_width)  11.2 us
    reshape x1, local copies, waits for them, and re-layouts, get_the_goods(): return jnp.concatenate(e_now, axis=array_dim)  10.4 us
  transfers between devices with their start and end apart: 5, of which 3 were waited for; matrix products, arithmetic and copies ran while one was open for 14% of the time, Pallas kernels for 0%

profile of v1, /device:TPU:0, one launch (start us, length us, event | category | flops | bytes accessed | tf_op | source)
XLA Modules:
  0.0 340.6 jit_solution(9019091004739077311)
XLA Ops:
  7.2 0.0 all-gather.5.cloned.1.call-start
  7.2 0.8 bitcast_or_fusion
  8.0 0.7 convert_reduce_fusion
  8.7 0.1 copy.139
  8.8 0.1 reshape.100
  8.9 0.1 fusion.80
  9.1 7.0 %gather_fusion.1 = f32[1024]{0:T(1024)S(1)} fusion(f32[128,16]{0,1:T(8,128)S(1)} %fusion.80, s32[1024]{0:T(1024)S(1)} %reshape.100), kind=kCustom, calls=%fused_computation.1 | custom fusion | bytes 16384 | tf_op jit(solution)/shard_map/jit(take_along_axis)/gather | solution.py:24
  16.1 0.1 reshape.103
  16.3 0.1 copy.141
  16.4 0.1 reshape.86
  16.5 5.6 %scatter_custom_fusion.1 = bf16[1536,512]{1,0:T(8,128)(2,1)S(1)} fusion(s32[1024]{0:T(1024)S(1)} %bitcast.193, bf16[]{:T(256)} %constant.14.clone.1, bf16[128,512]{1,0:T(8,128)(2,1)S(1)} %copy-done.13), kind=kCustom, calls=%fused_computation.78 | custom fusion | bytes 1703938 | tf_op jit(solution)/shard_map/scatter | solution.py:31
  22.1 44.3 %all_to_all.30 = bf16[8,192,512]{2,1,0:T(8,128)(2,1)} all-to-all(bf16[8,192,512]{2,1,0:T(8,128)(2,1)S(1)} %bitcast.191), channel_id=1, replica_groups=mesh['expert'=8,'tensor'=4] {'expert'}, dimensions={0} | all-to-all | bytes 3145728 | tf_op jit(solution)/shard_map/all_to_all | solution.py:66
  66.4 0.0 all-gather.5.cloned.1.call-update
  66.5 0.0 all-gather.3.cloned.1.call-start
  66.6 0.1 copy.142
  66.7 0.1 mul.92
  66.8 6.0 %scatter_custom_fusion = bf16[1536,512]{1,0:T(8,128)(2,1)S(1)} fusion(s32[1024]{0:T(1024)S(1)} %bitcast.194, f32[128,512]{1,0:T(8,128)S(1)} %convert_element_type.93, f32[1024]{0:T(1024)S(1)} %mul.92, bf16[]{:T(256)} %constant.14.clone.1), kind=kCustom, calls=%fused_computation.77 | custom fusion | flops 1048576 | bytes 1839106 | tf_op jit(solution)/shard_map/scatter | solution.py:31
  72.7 40.2 %all_to_all.31 = bf16[8,192,512]{2,1,0:T(8,128)(2,1)} all-to-all(bf16[8,192,512]{2,1,0:T(8,128)(2,1)S(1)} %bitcast.190), channel_id=1, replica_groups=mesh['expert'=8,'tensor'=4] {'expert'}, dimensions={0} | all-to-all | bytes 3145728 | tf_op jit(solution)/shard_map/all_to_all | solution.py:67
  112.9 0.0 all-gather.3.cloned.1.call-update
  113.0 0.2 reduce-scatter.2.cloned.1.call-start
  113.2 1.2 copy-done.4
  114.3 2.4 copy.135
  116.8 3.7 %copy.136 = bf16[2,2048,192]{2,1,0:T(8,128)(2,1)} copy(bf16[2,2048,192]{1,2,0:T(8,128)(2,1)} %param.18) | data formatting | bytes 3145728 | tf_op args[5]
  120.5 2.4 copy.137
  122.9 2.5 copy.138
  125.4 5.4 %fusion.37 = bf16[8,2,96,64]{2,3,0,1:T(8,128)(2,1)S(1)} fusion(bf16[2,2048,64]{1,2,0:T(8,128)(2,1)} %param.20, bf16[8,2,96,2048]{3,2,1,0:T(8,128)(2,1)} %bitcast.195), kind=kOutput, calls=%fused_computation.61 | convolution fusion | flops 402751488 | bytes 7012352 | tf_op jit(solution)/shard_map/mbtk,bkz->mbtz/dot_general | solution.py:78
  130.9 3.1 fusion.36
  134.0 3.1 fusion.14
  137.0 3.1 fusion.16
  140.1 19.9 %all-gather.3.cloned.1.call-done = bf16[4,1536,512]{2,1,0:T(8,128)(2,1)} async-done(((bf16[1,1536,512]{2,1,0:T(8,128)(2,1)}), bf16[4,1536,512]{2,1,0:T(8,128)(2,1)}) %all-gather.3.cloned.1.call-update) | async-done | bytes 6291472 | tf_op jit(solution)/shard_map/all_gather | solution.py:10
  159.9 10.4 %copy.143 = bf16[1536,4,512]{2,1,0:T(4,128)(2,1)} copy(bf16[1536,4,512]{2,0,1:T(8,128)(2,1)} %bitcast.187) | data formatting | bytes 12582912 | tf_op jit(solution)/shard_map/reshape | solution.py:11
  170.4 11.2 %reshape_reshape.3 = bf16[8,2,96,2048]{3,2,1,0:T(8,128)(2,1)} reshape(bf16[1536,4,512]{2,1,0:T(4,128)(2,1)} %copy.143) | data formatting | bytes 12582912 | tf_op jit(solution)/shard_map/reshape;reshape | solution.py:75
  181.5 5.3 %fusion.35 = bf16[8,2,96,64]{2,3,0,1:T(8,128)(2,1)S(1)} fusion(bf16[2,64,2048]{2,1,0:T(8,128)(2,1)S(1)} %copy-done.19, bf16[8,2,96,2048]{3,2,1,0:T(8,128)(2,1)} %reshape_reshape.3), kind=kOutput, calls=%fused_computation.59 | convolution fusion | flops 402751488 | bytes 7012352 | tf_op jit(solution)/shard_map/secd,erd->secr/dot_general | solution.py:106
  186.9 1.9 fusion.18
  188.9 0.4 multiply_add_fusion
  189.3 0.4 copy-done.10
  189.7 0.4 multiply_add_fusion.2
  190.1 0.5 copy-done.11
  190.7 0.6 copy-done.22
  191.2 1.1 fusion.27
  192.4 1.1 broadcast_multiply_fusion
  193.5 1.1 broadcast_multiply_fusion.1
  194.6 0.9 copy.150
  195.5 0.2 copy.151
  195.7 9.1 %convert_bitcast_fusion = bf16[8,2,96,2048]{3,2,0,1:T(8,128)(2,1)} fusion(bf16[2,2048,64]{2,1,0:T(8,128)(2,1)} %copy.138, bf16[2,2048,64]{2,1,0:T(8,128)(2,1)} %copy.137, bf16[2,2048,192]{2,1,0:T(8,128)(2,1)} %copy.136, bf16[2,2048,192]{2,1,0:T(8,128)(2,1)} %copy.135, bf16[8,2,96,64]{3,2,0,1:T(8,128)(2,1)S(1)} %copy.151, bf16[8,2,96,64]{3,2,0,1:T(8,128)(2,1)} %copy.150, ...), kind=kOutput, calls=%fused_computation.4 | convolution fusion | flops 3247439872 | bytes 12058624 | tf_op jit(solution)/shard_map/secf,edf->secd/dot_general | solution.py:141
  204.9 6.6 %copy.152 = bf16[8,2,96,2048]{3,2,1,0:T(8,128)(2,1)} copy(bf16[8,2,96,2048]{3,2,0,1:T(8,128)(2,1)} %convert_bitcast_fusion) | data formatting | bytes 12582912 | tf_op jit(solution)/shard_map/convert_element_type | solution.py:144
  211.4 0.0 reduce-scatter.2.cloned.1.call-update
  211.5 58.0 %reduce-scatter.2.cloned.1.call-done = bf16[1536,512]{1,0:T(8,128)(2,1)} async-done(((bf16[1536,2048]{1,0:T(8,128)(2,1)}), bf16[1536,512]{1,0:T(8,128)(2,1)}) %reduce-scatter.2.cloned.1.call-update) | async-done | bytes 1572880 | tf_op jit(solution)/shard_map/reduce_scatter | solution.py:183
  269.5 5.5 %all-to-all-start.2 = ((bf16[8,192,512]{2,1,0:T(8,128)(2,1)}), bf16[8,192,512]{2,1,0:T(8,128)(2,1)S(1)}, u32[]{:S(2)}, u32[]{:S(2)}) async-start(bf16[8,192,512]{2,1,0:T(8,128)(2,1)} %bitcast.192), calls=%async_computation.3 | async-start | bytes 3145728 | tf_op jit(solution)/shard_map/all_to_all | solution.py:189
  275.0 0.0 all-reduce.3.cloned.1.call-start
  275.0 0.1 copy.153
  275.1 0.1 reshape.94
  275.2 1.1 fusion.40
  276.4 0.0 all-reduce.3.cloned.1.call-update
  276.4 2.1 fusion.59
  278.5 1.9 fusion.60
  280.4 1.0 fusion.61
  281.4 32.6 %all-reduce.3.cloned.1.call-done = (bf16[8,2,96,64]{2,3,0,1:T(8,128)(2,1)}, bf16[8,2,96,64]{2,3,0,1:T(8,128)(2,1)}, bf16[8,2,96,64]{2,3,0,1:T(8,128)(2,1)}) async-done(((bf16[8,2,96,64]{2,3,0,1:T(8,128)(2,1)}, bf16[8,2,96,64]{2,3,0,1:T(8,128)(2,1)}, bf16[8,2,96,64]{2,3,0,1:T(8,128)(2,1)}), (bf16[8,2,96,64]{2,3,0,1:T(8,128)(2,1)}, bf16[8,2,96,64]{2,3,0,1:T(8,128)(2,1)}, ...) | async-done | bytes 589840 | tf_op jit(solution)/shard_map/psum | solution.py:148
  314.0 2.7 fusion.50
  316.7 2.6 fusion.56
  319.2 2.5 fusion.53
  321.8 2.2 bitcast_convert_fusion
  324.0 7.3 %gather_fusion = f32[1024,512]{1,0:T(8,128)} fusion(f32[1536,512]{1,0:T(8,128)} %bitcast_convert_fusion, s32[1024]{0:T(1024)S(1)} %broadcast_clamp_fusion), kind=kCustom, calls=%fused_computation | custom fusion | bytes 4198400 | tf_op jit(solution)/shard_map/gather | solution.py:192
  331.3 2.8 bitcast_reduce_fusion
  (49 shorter events, 0.2 us)
Async XLA Ops:
  7.2 179.7 %copy-start = (bf16[2,192,2048]{2,1,0:T(8,128)(2,1)S(1)}, bf16[2,192,2048]{2,1,0:T(8,128)(2,1)}, u32[]{:S(2)}) copy-start(bf16[2,192,2048]{2,1,0:T(8,128)(2,1)} %param.19) | copy-start | bytes 4718596
  7.2 118.3 %all-gather.5.cloned.1.call-start = ((), (), s32[]{:S(2)}) async-start(), calls=%async_computation.5 | async-start | bytes 7864320 | tf_op jit(solution)/shard_map/all_gather | solution.py:70
  9.1 7.2 %copy-start.16 = (s32[128,8]{0,1:T(8,128)S(1)}, s32[128,8]{0,1:T(8,128)}, u32[]{:S(2)}) copy-start(s32[128,8]{0,1:T(8,128)} %param.16) | copy-start | bytes 12292
  9.1 7.4 %copy-start.13 = (bf16[128,512]{1,0:T(8,128)(2,1)S(1)}, bf16[128,512]{1,0:T(8,128)(2,1)}, u32[]{:S(2)}) copy-start(bf16[128,512]{1,0:T(8,128)(2,1)} %param.13) | copy-start | bytes 393220
  22.1 44.4 %copy-start.14 = (bf16[128,512]{1,0:T(8,128)(2,1)S(1)}, bf16[128,512]{1,0:T(8,128)(2,1)}, u32[]{:S(2)}) copy-start(bf16[128,512]{1,0:T(8,128)(2,1)} %param.14) | copy-start | bytes 393220
  22.1 44.5 %copy-start.17 = (f32[128,8]{0,1:T(8,128)S(1)}, f32[128,8]{0,1:T(8,128)}, u32[]{:S(2)}) copy-start(f32[128,8]{0,1:T(8,128)} %param.15) | copy-start | bytes 12292
  66.5 93.5 %all-gather.3.cloned.1.call-start = ((), (), s32[]{:S(2)}) async-start(), calls=%async_computation.4 | async-start | bytes 7864320 | tf_op jit(solution)/shard_map/all_gather | solution.py:10
  112.9 1.4 copy-start.4
  113.0 156.5 %reduce-scatter.2.cloned.1.call-start = ((), (), s32[]{:S(2)}) async-start(), calls=%async_computation.6 | async-start | bytes 7864320 | tf_op jit(solution)/shard_map/reduce_scatter | solution.py:183
  125.4 5.4 %copy-start.9 = (bf16[2,2048,64]{1,2,0:T(8,128)(2,1)S(1)}, bf16[2,2048,64]{1,2,0:T(8,128)(2,1)}, u32[]{:S(2)}) copy-start(bf16[2,2048,64]{1,2,0:T(8,128)(2,1)} %param.22) | copy-start | bytes 1572868
  125.4 5.4 %copy-start.18 = (bf16[1536,2048]{1,0:T(8,128)(2,1)S(1)}, bf16[1536,2048]{1,0:T(8,128)(2,1)}, u32[]{:S(2)}) copy-start(bf16[1536,2048]{1,0:T(8,128)(2,1)} %all-gather.5.cloned.1.call-done) | copy-start | bytes 18874372
  134.0 3.1 copy-start.5
  170.4 11.2 %copy-start.19 = (bf16[2,64,2048]{2,1,0:T(8,128)(2,1)S(1)}, bf16[2,64,2048]{2,1,0:T(8,128)(2,1)}, u32[]{:S(2)}) copy-start(bf16[2,64,2048]{2,1,0:T(8,128)(2,1)} %param.25) | copy-start | bytes 1572868
  181.5 5.3 %copy-start.2 = (bf16[8,2,96,2048]{3,2,1,0:T(8,128)(2,1)S(1)}, bf16[8,2,96,2048]{3,2,1,0:T(8,128)(2,1)}, u32[]{:S(2)}) copy-start(bf16[8,2,96,2048]{3,2,1,0:T(8,128)(2,1)} %reshape_reshape.3) | copy-start | bytes 18874372
  186.9 2.4 copy-start.7
  186.9 1.9 copy-start.6
  186.9 1.9 copy-start.12
  188.9 0.8 copy-start.10
  189.7 0.9 copy-start.11
  189.7 1.0 copy-start.15
  189.7 1.5 copy-start.22
  192.3 12.5 %copy-start.3 = (bf16[8,2,96,192]{3,2,0,1:T(8,128)(2,1)}, bf16[8,2,96,192]{3,2,0,1:T(8,128)(2,1)S(1)}, u32[]{:S(2)}) copy-start(bf16[8,2,96,192]{3,2,0,1:T(8,128)(2,1)S(1)} %get-tuple-element.13) | copy-start | bytes 1769476
  269.5 52.3 %all-to-all-start.2 = ((bf16[8,192,512]{2,1,0:T(8,128)(2,1)}), bf16[8,192,512]{2,1,0:T(8,128)(2,1)S(1)}, u32[]{:S(2)}, u32[]{:S(2)}) async-start(bf16[8,192,512]{2,1,0:T(8,128)(2,1)} %bitcast.192), calls=%async_computation.3 | async-start | bytes 3145728 | tf_op jit(solution)/shard_map/all_to_all | solution.py:189
  275.0 39.0 %all-reduce.3.cloned.1.call-start = ((), (), s32[]{:S(2)}) async-start(), calls=%async_computation.7 | async-start | bytes 1572864 | tf_op jit(solution)/shard_map/psum | solution.py:148
  276.4 4.0 %copy-start.8 = (bf16[8,2,96,64]{2,3,0,1:T(8,128)(2,1)S(1)}, bf16[8,2,96,64]{2,3,0,1:T(8,128)(2,1)}, u32[]{:S(2)}) copy-start(bf16[8,2,96,64]{2,3,0,1:T(8,128)(2,1)} %copy-done.7) | copy-start | bytes 589828
  314.0 2.7 copy-start.21
  316.6 2.6 copy-start.20
  324.0 10.1 %copy-start.1 = (bf16[2,192,2048]{2,1,0:T(8,128)(2,1)S(1)}, bf16[2,192,2048]{2,1,0:T(8,128)(2,1)}, u32[]{:S(2)}) copy-start(bf16[2,192,2048]{2,1,0:T(8,128)(2,1)} %param.19) | copy-start | bytes 4718596
Sparse Core Ops, SparseCore 0:
  66.6 45.3 all-gather.4
  113.6 46.3 all-gather.2
  211.6 57.8 reduce-scatter.1
  278.6 35.3 all-reduce.2
